TPU v7x, 32 devices: a whole 2x2x4 slice. The times are simulated.
32 devices in a mesh: node: 16 (over z, y, core), blk: 2 (over x).
Axes of the slice: x: 2, y: 2, z: 4, core: 2. Of those that a mesh axis runs over, the one named last changes fastest.
Arguments:
- params: bfloat16 [16, 128, 14336], P('node', 'blk'), may hold values from -40 to 40
- weights: int32 [16], P('node'), may hold values from 1 to 8
Outputs:
- debiased: float32 [16, 128, 14336], P('node', 'blk')
- average: float32 [128, 14336], P('blk', 'node')
- spread: float32 [16], P('node')
All inputs are finite; a program needn't handle non-finite values.
Results may differ from a plain program's by a relative error of at most 0.0003.
Values may be sent and summed in bfloat16 or wider, within the bound.
A program may use at most 64 MiB of HBM per device.

v0:
```python
import jax
import jax.numpy as jnp
from jax import lax
from jax.sharding import PartitionSpec as P

ROUNDS = 3


def from_behind(value, axis, steps):
    count = lax.axis_size(axis)
    pairs = [(source, (source + steps) % count) for source in range(count)]
    return lax.ppermute(value, axis, pairs)


def push_round(value, scale, hop):
    received = from_behind((value, scale), "node", hop)
    return (received[0], received[1])


def shards(params, weights):
    node_count = lax.axis_size("node")
    levels = node_count.bit_length() - 1
    scale0 = weights.astype(jnp.float32)
    weighted = scale0[:, None, None] * params.astype(jnp.float32)
    value = weighted
    scale = scale0
    for step in range(ROUNDS):
        hop = 1 << step % levels
        if step == 0:
            raw = from_behind((params, weights.astype(jnp.bfloat16)), "node", hop)
            other_scale = raw[1].astype(jnp.float32)
            other_value = other_scale[:, None, None] * raw[0].astype(jnp.float32)
        else:
            other_value, other_scale = push_round(value, scale, hop)
        value = 0.5 * value + 0.5 * other_value
        scale = 0.5 * scale + 0.5 * other_scale
    debiased = value / scale[:, None, None]
    hidden_units = params.shape[2]
    width = hidden_units // node_count
    local = debiased[0]
    numer, total = lax.psum((weighted[0], jnp.sum(scale0)), "node")
    whole = numer / total
    partial_value = jnp.sum((local - whole) ** 2)[None]
    average = lax.dynamic_slice_in_dim(whole, lax.axis_index("node") * width, width, 1)
    row_count = params.shape[1] * lax.axis_size("blk")
    spread = lax.psum(partial_value, "blk") / (row_count * hidden_units)
    return (debiased, average, spread)


def solution(mesh):
    return jax.shard_map(
        shards,
        mesh=mesh,
        in_specs=(P("node", "blk", None), P("node")),
        out_specs=(P("node", "blk", None), P("blk", "node"), P("node")),
        check_vma=False,
    )
```

profile of v0, /device:TPU:0, one launch (start us, length us, event | category | flops | bytes accessed | tf_op | source)
XLA Modules:
  0.0 320.9 jit_solution(3356711816750203309)
XLA Ops:
  7.2 0.0 all-reduce.2.cloned.1.call-start
  7.2 0.5 collective-permute-start.1
  8.4 3.6 %collective-permute-start = (bf16[1]{0:T(256)(128)(2,1)}, bf16[1]{0:T(256)(128)(2,1)}, u32[]{:S(2)}, u32[]{:S(2)}) collective-permute-start(bf16[1]{0:T(256)(128)(2,1)} %convert_element_type.17), channel_id=1, source_target_pairs={{0,2},{2,4},{4,6},{6,8},{8,10},{10,12},{12,14},{14,16},{16,18},{18... | collective-permute-start | bytes 14 | tf_op jit(solution)/shard_map/ppermute | solution.py:12
  12.0 21.9 %collective-permute-done = bf16[1]{0:T(256)(128)(2,1)} collective-permute-done((bf16[1]{0:T(256)(128)(2,1)}, bf16[1]{0:T(256)(128)(2,1)}, u32[]{:S(2)}, u32[]{:S(2)}) %collective-permute-start) | collective-permute-done | bytes 34 | tf_op jit(solution)/shard_map/ppermute | solution.py:12
  34.6 0.0 collective-permute-done.1
  34.6 0.0 copy-start
  34.6 2.3 fusion.3
  37.0 0.1 collective-permute-start.2
  37.0 80.8 %collective-permute-done.2 = f32[1,64,14336]{2,1,0:T(8,128)S(1)} collective-permute-done((f32[1,64,14336]{2,1,0:T(8,128)S(1)}, f32[1,64,14336]{2,1,0:T(8,128)S(1)}, u32[]{:S(2)}, u32[]{:S(2)}) %collective-permute-start.2) | collective-permute-done | bytes 3670048 | tf_op jit(solution)/shard_map/ppermute | solution.py:12
  117.9 0.0 copy-done
  117.9 4.0 %multiply_add_fusion = (f32[1,64,14336]{2,1,0:T(8,128)}, f32[64,14336]{1,0:T(8,128)}) fusion(f32[1,64,14336]{2,1,0:T(8,128)S(1)} %collective-permute-done.2, bf16[1,64,14336]{2,1,0:T(8,128)(2,1)S(1)} %collective-permute-done.1, bf16[1,64,14336]{2,1,0:T(8,128)(2,1)S(1)} %copy-done, f32[]{:T(128)} %bitcast.1, f32[]{:T(128)} %bitcast), kind=kLoop, calls=%fused_computation.4 | loop fusion | flops 7340032 | bytes 14680072 | tf_op jit(solution)/shard_map/add | solution.py:35
  121.9 0.0 collective-permute-start.3
  121.9 0.0 all-reduce.2.cloned.1.call-update
  121.9 127.2 %psum.22 = f32[]{:T(128)} all-reduce(f32[]{:T(128)} %bitcast), channel_id=1, replica_groups=mesh['node'=16,'blk'=2] {'node'}, use_global_device_ids=true, to_apply=%region_1.0 | all-reduce | flops 1 | bytes 8 | tf_op jit(solution)/shard_map/psum | solution.py:41
  249.8 1.4 collective-permute-start.4
  251.1 5.1 %collective-permute-done.4 = f32[1]{0:T(128)} collective-permute-done((f32[1]{0:T(128)}, f32[1]{0:T(128)}, u32[]{:S(2)}, u32[]{:S(2)}) %collective-permute-start.4) | collective-permute-done | bytes 36 | tf_op jit(solution)/shard_map/ppermute | solution.py:12
  256.8 1.4 collective-permute-start.5
  258.2 4.2 %collective-permute-done.5 = f32[1]{0:T(128)} collective-permute-done((f32[1]{0:T(128)}, f32[1]{0:T(128)}, u32[]{:S(2)}, u32[]{:S(2)}) %collective-permute-start.5) | collective-permute-done | bytes 36 | tf_op jit(solution)/shard_map/ppermute | solution.py:12
  263.0 32.3 %all-reduce.2.cloned.1.call-done = f32[64,14336]{1,0:T(8,128)} async-done(((f32[64,14336]{1,0:T(8,128)}), f32[64,14336]{1,0:T(8,128)}) %all-reduce.2.cloned.1.call-update) | async-done | bytes 3670032 | tf_op jit(solution)/shard_map/psum | solution.py:41
  295.3 0.0 collective-permute-done.3
  295.3 9.8 %fusion.1 = (f32[]{:T(128)}, f32[64,14336]{1,0:T(8,128)}, f32[1,64,14336]{2,1,0:T(8,128)}) fusion(f32[64,14336]{1,0:T(8,128)} %all-reduce.2.cloned.1.call-done, f32[]{:T(128)} %psum.22, f32[]{:T(128)} %bitcast.2, f32[1,64,14336]{2,1,0:T(8,128)} %get-tuple-element.6, f32[1,64,14336]{2,1,0:T(8,128)} %collective-permute-done.3), kind=kLoop, calls=%fused_computation.2 | loop fusion | flops 6422527 | bytes 18350092 | tf_op jit(solution)/shard_map/reduce_sum | solution.py:43
  305.1 5.5 %psum.23 = f32[1]{0:T(128)} all-reduce(f32[1]{0:T(128)} %bitcast.5), channel_id=1, replica_groups=mesh['node'=16,'blk'=2] {'blk'}, use_global_device_ids=true, to_apply=%region_3.0 | all-reduce | flops 1 | bytes 8 | tf_op jit(solution)/shard_map/psum | solution.py:46
  310.6 1.6 constant_dynamic-slice_fusion
Async XLA Ops:
  7.2 288.1 %all-reduce.2.cloned.1.call-start = ((), (), s32[]{:S(2)}) async-start(), calls=%async_computation | async-start | bytes 7340032 | tf_op jit(solution)/shard_map/psum | solution.py:41
  7.2 27.4 %collective-permute-start.1 = (bf16[1,64,14336]{2,1,0:T(8,128)(2,1)}, bf16[1,64,14336]{2,1,0:T(8,128)(2,1)S(1)}, u32[]{:S(2)}, u32[]{:S(2)}) collective-permute-start(bf16[1,64,14336]{2,1,0:T(8,128)(2,1)} %param.2), channel_id=1, source_target_pairs={{0,2},{2,4},{4,6},{6,8},{8,10},{10,12},{12,14},{14,16},{16,18},{18... | collective-permute-start | bytes 5505032 | tf_op jit(solution)/shard_map/ppermute | solution.py:12
  8.4 25.6 %collective-permute-start = (bf16[1]{0:T(256)(128)(2,1)}, bf16[1]{0:T(256)(128)(2,1)}, u32[]{:S(2)}, u32[]{:S(2)}) collective-permute-start(bf16[1]{0:T(256)(128)(2,1)} %convert_element_type.17), channel_id=1, source_target_pairs={{0,2},{2,4},{4,6},{6,8},{8,10},{10,12},{12,14},{14,16},{16,18},{18... | collective-permute-start | bytes 14 | tf_op jit(solution)/shard_map/ppermute | solution.py:12
  34.6 83.2 %copy-start = (bf16[1,64,14336]{2,1,0:T(8,128)(2,1)S(1)}, bf16[1,64,14336]{2,1,0:T(8,128)(2,1)}, u32[]{:S(2)}) copy-start(bf16[1,64,14336]{2,1,0:T(8,128)(2,1)} %param.2) | copy-start | bytes 5505028
  37.0 80.9 %collective-permute-start.2 = (f32[1,64,14336]{2,1,0:T(8,128)S(1)}, f32[1,64,14336]{2,1,0:T(8,128)S(1)}, u32[]{:S(2)}, u32[]{:S(2)}) collective-permute-start(f32[1,64,14336]{2,1,0:T(8,128)S(1)} %fusion.3), channel_id=1, source_target_pairs={{0,4},{2,6},{4,8},{6,10},{8,12},{10,14},{12,16},{14,18},{16,20},{1... | collective-permute-start | bytes 11010056 | tf_op jit(solution)/shard_map/ppermute | solution.py:12
  121.9 173.4 %collective-permute-start.3 = (f32[1,64,14336]{2,1,0:T(8,128)}, f32[1,64,14336]{2,1,0:T(8,128)}, u32[]{:S(2)}, u32[]{:S(2)}) collective-permute-start(f32[1,64,14336]{2,1,0:T(8,128)} %get-tuple-element.6), channel_id=1, source_target_pairs={{0,8},{2,10},{4,12},{6,14},{8,16},{10,18},{12,20},{14,22},{16,24},... | collective-permute-start | bytes 11010056 | tf_op jit(solution)/shard_map/ppermute | solution.py:12
  249.8 6.4 %collective-permute-start.4 = (f32[1]{0:T(128)}, f32[1]{0:T(128)}, u32[]{:S(2)}, u32[]{:S(2)}) collective-permute-start(f32[1]{0:T(128)} %add.34), channel_id=1, source_target_pairs={{0,4},{2,6},{4,8},{6,10},{8,12},{10,14},{12,16},{14,18},{16,20},{1... | collective-permute-start | bytes 20 | tf_op jit(solution)/shard_map/ppermute | solution.py:12
  256.8 5.5 %collective-permute-start.5 = (f32[1]{0:T(128)}, f32[1]{0:T(128)}, u32[]{:S(2)}, u32[]{:S(2)}) collective-permute-start(f32[1]{0:T(128)} %add.35), channel_id=1, source_target_pairs={{0,8},{2,10},{4,12},{6,14},{8,16},{10,18},{12,20},{14,22},{16,24},... | collective-permute-start | bytes 20 | tf_op jit(solution)/shard_map/ppermute | solution.py:12
Sparse Core Ops, SparseCore 0:
  122.0 173.2 all-reduce.1
where the time goes:
time: 321 us
  waiting for transfers between devices  144 us (45%)
  blocking collectives  133 us (41%)
  between operations  19 us (6%)
  other arithmetic  16.2 us (5%)
  starting transfers between devices  6.97 us (2%)
    psum x1, blocking collectives, shards(): numer, total = lax.psum((weighted[0], jnp.sum(scale0)), 'node')  127 us
    ppermute x6, waiting for transfers between devices, from_behind(): return lax.ppermute(value, axis, pairs)  112 us
    psum x1, waiting for transfers between devices, shards(): numer, total = lax.psum((weighted[0], jnp.sum(scale0)), 'node')  32.3 us
    reduce_sum x1, other arithmetic, shards(): partial_value = jnp.sum((local - whole) ** 2)[None]  9.8 us
    ppermute x6, starting transfers between devices, from_behind(): return lax.ppermute(value, axis, pairs)  6.94 us
  transfers between devices with their start and end apart: 7, of which 5 were waited for; matrix products, arithmetic and copies ran while one was open for 0% of the time, Pallas kernels for 0%

commit v1 on v0

--- a/solution.py
+++ b/solution.py
@@ -1,9 +1,370 @@
+import functools
+
 import jax
 import jax.numpy as jnp
 from jax import lax
+from jax.experimental import pallas as pl
+from jax.experimental.pallas import tpu as pltpu
 from jax.sharding import PartitionSpec as P
 
 ROUNDS = 3
+GROUP = 4
+LEVELS = 4
+SPLIT = 2
+LANES = 128
+
+
+def kernel(p_ref, w_ref, out_ref, avg_ref, spread_ref,
+           raw_own, raw_a, raw_b, raw_c, q_a, q_b, q_send, dbuf, avgbuf,
+           wts, acc, spread_in, spread_part, spread_x,
+           near_send, near_recv, own_sem, far_send, far_recv, back_send, back_recv,
+           back_own, w_send, w_recv, s_send, s_recv, avg_sem):
+    node = lax.axis_index("node")
+    side = lax.axis_index("blk")
+    z = node // GROUP
+    r = node % GROUP
+    half, core = r // 2, r % 2
+    rows, width = raw_own.shape[2], raw_own.shape[3]
+    chunks = raw_own.shape[0]
+    hidden = p_ref.shape[2]
+    row_total = p_ref.shape[1] * lax.axis_size("blk")
+
+    def peer(o):
+        y = 1 - half if o & 2 else half
+        c = 1 - core if o & 1 else core
+        return y * 2 + c
+
+    def dev(zz, rr):
+        return {"node": zz * GROUP + rr}
+
+    inner = jnp.logical_and(z >= 1, z <= 2)
+    outer = jnp.logical_not(inner)
+    mate = 3 - z
+    nb = (z // 2) * 2 + 1 - z % 2
+    inner_count = (1 - z // 3) * ((z + 2) // 3)
+    opposite = (z + 2) % LEVELS
+    behind = (z + 3) % LEVELS
+
+    def remote(src, dst, ssem, rsem, device):
+        return pltpu.make_async_remote_copy(
+            src_ref=src, dst_ref=dst, send_sem=ssem, recv_sem=rsem,
+            device_id=device, device_id_type=pl.DeviceIdType.MESH)
+
+    wts[z, r] = jnp.full((8, LANES), w_ref[0].astype(jnp.float32))
+    acc[...] = jnp.zeros_like(acc)
+
+    def own_slice(k):
+        return pl.ds((k % SPLIT) * rows, rows)
+
+    def block(k, rr):
+        return pl.ds(pl.multiple_of(((k // SPLIT) * GROUP + rr) * width, LANES), width)
+
+    locals_in = []
+    for k in range(chunks):
+        locals_in.append(pltpu.make_async_copy(
+            p_ref.at[0, own_slice(k), block(k, r)], raw_own.at[k, r], own_sem.at[k]))
+        locals_in[-1].start()
+
+    barrier = pltpu.get_barrier_semaphore()
+
+    def greet(device):
+        pl.semaphore_signal(barrier, inc=1, device_id=device,
+                            device_id_type=pl.DeviceIdType.MESH)
+
+    for o in (1, 2, 3):
+        greet(dev(z, peer(o)))
+    greet({"blk": 1 - side})
+    greet(dev(nb, r))
+
+    @pl.when(inner)
+    def _():
+        greet(dev(mate, r))
+
+    pl.semaphore_wait(barrier, 5 + inner_count)
+
+    def w_near(o):
+        return remote(wts.at[z, r], wts.at[z, r], w_send.at[o - 1], w_recv.at[o - 1],
+                      dev(z, peer(o)))
+
+    def near(k, o):
+        return remote(p_ref.at[0, own_slice(k), block(k, peer(o))], raw_own.at[k, r],
+                      near_send.at[k, o - 1], near_recv.at[k, o - 1], dev(z, peer(o)))
+
+    for o in (1, 2, 3):
+        w_near(o).start()
+    for k in range(chunks):
+        for o in (2, 3, 1):
+            near(k, o).start()
+
+    arrived = set()
+
+    def wait_own(k):
+        if k in arrived:
+            return
+        arrived.add(k)
+        locals_in[k].wait()
+        for o in (1, 2, 3):
+            near(k, o).wait_recv()
+
+    def row(zz, i):
+        return wts[zz, i, 0:1, :]
+
+    def f32(ref, k, i, cols):
+        return ref[k, i, :, cols].astype(jnp.float32)
+
+    def group_sum(ref, k, zz, cols):
+        total = f32(ref, k, 0, cols) * row(zz, 0)
+        for i in range(1, GROUP):
+            total = total + f32(ref, k, i, cols) * row(zz, i)
+        return total
+
+    def columns(j):
+        return pl.ds(pl.multiple_of(j * LANES, LANES), LANES)
+
+    def back(k, o):
+        return remote(dbuf.at[k, peer(o)], out_ref.at[0, own_slice(k), block(k, r)],
+                      back_send.at[k, o - 1], back_recv.at[k, o - 1], dev(z, peer(o)))
+
+    def back_local(k):
+        return pltpu.make_async_copy(
+            dbuf.at[k, r], out_ref.at[0, own_slice(k), block(k, r)], back_own.at[k])
+
+    def group_weight(zz):
+        return row(zz, 0) + row(zz, 1) + row(zz, 2) + row(zz, 3)
+
+    def finish(k, is_inner):
+        far = raw_c if is_inner else raw_a
+        at_one = (z == 1)
+        at_zero = (z == 0)
+        s0, s1 = row(z, 0), row(z, 0) + row(z, 1)
+        s2 = s1 + row(z, 2)
+        s3 = s2 + row(z, 3)
+        t3 = row(opposite, 3)
+        t2 = t3 + row(opposite, 2)
+        t1 = t2 + row(opposite, 1)
+        sb = group_weight(behind)
+        scales = (1.0 / (s0 + sb + t1), 1.0 / (s1 + sb + t2), 1.0 / (s2 + sb + t3),
+                  1.0 / (s3 + sb))
+        whole = 1.0 / (group_weight(0) + group_weight(1) + group_weight(2) + group_weight(3))
+
+        def step(j, sums):
+            cols = columns(j)
+            v0 = f32(raw_own, k, 0, cols) * row(z, 0)
+            v1 = v0 + f32(raw_own, k, 1, cols) * row(z, 1)
+            v2 = v1 + f32(raw_own, k, 2, cols) * row(z, 2)
+            v3 = v2 + f32(raw_own, k, 3, cols) * row(z, 3)
+            u3 = f32(far, k, 3, cols) * row(opposite, 3)
+            u2 = u3 + f32(far, k, 2, cols) * row(opposite, 2)
+            u1 = u2 + f32(far, k, 1, cols) * row(opposite, 1)
+            u0 = u1 + f32(far, k, 0, cols) * row(opposite, 0)
+            if is_inner:
+                q_send[k, 1, :, cols] = u0
+                qo = group_sum(raw_a, k, nb, cols)
+                qj = group_sum(raw_b, k, mate, cols)
+                prior = jnp.where(at_one, qo, qj)
+                total = v3 + u0 + qo + qj
+            else:
+                qi = q_a[k, :, cols]
+                qx = q_b[k, :, cols]
+                prior = jnp.where(at_zero, qx, qi)
+                total = v3 + u0 + qi + qx
+            mean = total * whole
+            avgbuf[k // SPLIT, own_slice(k), cols] = mean
+            fresh = []
+            for i, value in enumerate((v0 + u1, v1 + u2, v2 + u3, v3)):
+                d = (value + prior) * scales[i]
+                dbuf[k, i, :, cols] = d
+                gap = d - mean
+                gap = gap * gap
+                part = gap[0:8]
+                for e in range(8, rows, 8):
+                    part = part + gap[e:e + 8]
+                fresh.append(sums[i] + part)
+            return tuple(fresh)
+
+        zero = jnp.zeros((8, LANES), jnp.float32)
+        sums = lax.fori_loop(0, width // LANES, step, (zero,) * GROUP)
+        for i in range(GROUP):
+            acc[i] += sums[i]
+
+    def send_back(k):
+        for o in (2, 3, 1):
+            back(k, o).start()
+        back_local(k).start()
+
+    def to_inner(k):
+        return remote(raw_own.at[k], raw_a.at[k], far_send.at[k, 0], far_recv.at[k, 0],
+                      dev(nb, r))
+
+    def across(k):
+        return remote(raw_own.at[k], raw_b.at[k], far_send.at[k, 0], far_recv.at[k, 1],
+                      dev(mate, r))
+
+    def across_relay(k):
+        return remote(raw_a.at[k], raw_c.at[k], far_send.at[k, 1], far_recv.at[k, 2],
+                      dev(mate, r))
+
+    def outward_relay(k):
+        return remote(raw_b.at[k], raw_a.at[k], far_send.at[k, 2], far_recv.at[k, 0],
+                      dev(nb, r))
+
+    def outward_q(k, which):
+        dst = q_b if which else q_a
+        return remote(q_send.at[k, which], dst.at[k], far_send.at[k, 3 + which],
+                      far_recv.at[k, 3 + which], dev(nb, r))
+
+    def w_copy(level, slot, target):
+        return remote(wts.at[level], wts.at[level], w_send.at[slot], w_recv.at[slot],
+                      dev(target, r))
+
+    def wait_weights():
+        for o in (1, 2, 3):
+            w_near(o).wait_recv()
+
+    @pl.when(inner)
+    def _():
+        arrived.clear()
+
+        def group_out(k):
+            wait_own(k)
+
+            def step(j, carry):
+                cols = columns(j)
+                q_send[k, 0, :, cols] = group_sum(raw_own, k, z, cols)
+                return carry
+
+            lax.fori_loop(0, width // LANES, step, 0)
+            outward_q(k, 0).start()
+
+        wait_weights()
+        w_copy(z, 3, nb).start()
+        w_copy(z, 4, mate).start()
+        for t in range(chunks + 2):
+            if t < chunks:
+                wait_own(t)
+                across(t).start()
+            for k in ((0,) if t == 0 else (2 * t - 1, 2 * t)):
+                if k < chunks:
+                    group_out(k)
+            if t == 1:
+                w_copy(nb, 3, nb).wait_recv()
+                w_copy(nb, 5, mate).start()
+                w_copy(z, 4, mate).wait_recv()
+                w_copy(mate, 6, nb).start()
+            k = t - 1
+            if 0 <= k < chunks:
+                across_in = to_inner(k)
+                across_in.wait_recv()
+                across_relay(k).start()
+                across(k).wait_recv()
+                outward_relay(k).start()
+            if t == 2:
+                w_copy(nb, 5, mate).wait_recv()
+                w_copy(opposite, 7, nb).start()
+            k = t - 2
+            if 0 <= k < chunks:
+                across_relay(k).wait_recv()
+                finish(k, True)
+                send_back(k)
+                outward_q(k, 1).start()
+        for k in range(chunks):
+            across(k).wait_send()
+            across_relay(k).wait_send()
+            outward_relay(k).wait_send()
+            outward_q(k, 0).wait_send()
+            outward_q(k, 1).wait_send()
+        w_copy(z, 3, nb).wait_send()
+        w_copy(z, 4, mate).wait_send()
+        w_copy(nb, 5, mate).wait_send()
+        w_copy(mate, 6, nb).wait_send()
+        w_copy(opposite, 7, nb).wait_send()
+
+    @pl.when(outer)
+    def _():
+        arrived.clear()
+        wait_weights()
+        w_copy(z, 3, nb).start()
+        for k in range(chunks):
+            wait_own(k)
+            to_inner(k).start()
+        w_copy(nb, 3, nb).wait_recv()
+        w_copy(opposite, 6, nb).wait_recv()
+        w_copy(mate, 7, nb).wait_recv()
+        for k in range(chunks):
+            outward_q(k, 0).wait_recv()
+            outward_relay(k).wait_recv()
+            outward_q(k, 1).wait_recv()
+            finish(k, False)
+            send_back(k)
+        for k in range(chunks):
+            to_inner(k).wait_send()
+        w_copy(z, 3, nb).wait_send()
+
+    average = pltpu.make_async_copy(avgbuf.at[z], avg_ref, avg_sem)
+    average.start()
+
+    def share(o):
+        return remote(acc.at[peer(o)], spread_in.at[o - 1], s_send.at[o - 1],
+                      s_recv.at[o - 1], dev(z, peer(o)))
+
+    for o in (1, 2, 3):
+        share(o).start()
+    for o in (1, 2, 3):
+        share(o).wait_recv()
+    spread_part[...] = acc[r] + spread_in[0] + spread_in[1] + spread_in[2]
+    swap = remote(spread_part, spread_x, s_send.at[3], s_recv.at[3], {"blk": 1 - side})
+    swap.start()
+    for k in range(chunks):
+        for o in (1, 2, 3):
+            near(k, o).wait_send()
+            back(k, o).wait()
+        back_local(k).wait()
+    for o in (1, 2, 3):
+        w_near(o).wait_send()
+        share(o).wait_send()
+    average.wait()
+    swap.wait()
+    spread_ref[0] = jnp.sum(spread_part[...] + spread_x[...]) / (row_total * hidden)
+
+
+def fused(params, weights):
+    _, rows, hidden = params.shape
+    node_count = lax.axis_size("node")
+    width = hidden // node_count
+    piece = rows // SPLIT
+    chunks = LEVELS * SPLIT
+    raw = pltpu.VMEM((chunks, GROUP, piece, width), params.dtype)
+    q = pltpu.VMEM((chunks, piece, width), jnp.float32)
+    tile = pltpu.VMEM((8, LANES), jnp.float32)
+    dma = pltpu.SemaphoreType.DMA
+    debiased, average, spread = pl.pallas_call(
+        kernel,
+        out_shape=(
+            jax.ShapeDtypeStruct((1, rows, hidden), jnp.float32),
+            jax.ShapeDtypeStruct((rows, width), jnp.float32),
+            jax.ShapeDtypeStruct((1,), jnp.float32),
+        ),
+        in_specs=[pl.BlockSpec(memory_space=pl.ANY), pl.BlockSpec(memory_space=pltpu.SMEM)],
+        out_specs=(pl.BlockSpec(memory_space=pl.ANY), pl.BlockSpec(memory_space=pl.ANY),
+                   pl.BlockSpec(memory_space=pltpu.SMEM)),
+        scratch_shapes=[
+            raw, raw, raw, raw, q, q,
+            pltpu.VMEM((chunks, 2, piece, width), jnp.float32),
+            pltpu.VMEM((chunks, GROUP, piece, width), jnp.float32),
+            pltpu.VMEM((LEVELS, rows, width), jnp.float32),
+            pltpu.VMEM((LEVELS, GROUP, 8, LANES), jnp.float32),
+            pltpu.VMEM((GROUP, 8, LANES), jnp.float32),
+            pltpu.VMEM((3, 8, LANES), jnp.float32),
+            tile, tile,
+            dma((chunks, 3)), dma((chunks, 3)), dma((chunks,)),
+            dma((chunks, 5)), dma((chunks, 5)),
+            dma((chunks, 3)), dma((chunks, 3)), dma((chunks,)),
+            dma((8,)), dma((8,)), dma((4,)), dma((4,)), dma,
+        ],
+        compiler_params=pltpu.CompilerParams(
+            collective_id=0, has_side_effects=True, vmem_limit_bytes=56 << 20),
+    )(params, weights)
+    return debiased, average, spread
 
 
 def from_behind(value, axis, steps):
@@ -48,8 +409,9 @@
 
 
 def solution(mesh):
+    line = mesh.shape["node"] == GROUP * LEVELS and mesh.shape["blk"] == 2
     return jax.shard_map(
-        shards,
+        fused if line else shards,
         mesh=mesh,
         in_specs=(P("node", "blk", None), P("node")),
         out_specs=(P("node", "blk", None), P("blk", "node"), P("node")),

time: 321 us -> 116 us (0.36)
  waiting for transfers between devices: 144 us -> 0 us
  blocking collectives: 133 us -> 0 us
  Pallas kernels: 0 us -> 108 us
  other arithmetic: 16.2 us -> 0 us
  between operations: 19 us -> 3.05 us
  starting transfers between devices: 6.97 us -> 0 us
  local copies, waits for them, and re-layouts: 1.64 us -> 4.87 us
    psum x2 -> x0, blocking collectives: 133 us -> none  [the longest x1 127 us: shards(): numer, total = lax.psum((weighted[0], jnp.sum(scale0)), 'node')]
    ppermute x6 -> x0, waiting for transfers between devices: 112 us -> none  [from_behind(): return lax.ppermute(value, axis, pairs)]
    pallas_call x0 -> x1, Pallas kernels: none -> 108 us  [fused(): pl.pallas_call(kernel, out_shape=(jax.ShapeDtypeStruct((1, rows, hidden),...]
    psum x1 -> x0, waiting for transfers between devices: 32.3 us -> none  [shards(): numer, total = lax.psum((weighted[0], jnp.sum(scale0)), 'node')]
    reduce_sum x1 -> x0, other arithmetic: 9.8 us -> none  [shards(): partial_value = jnp.sum((local - whole) ** 2)[None]]
    ppermute x6 -> x0, starting transfers between devices: 6.94 us -> none  [from_behind(): return lax.ppermute(value, axis, pairs)]
    add x2 -> x0, other arithmetic: 6.37 us -> none  [shards(): value = 0.5 * value + 0.5 * other_value]
    unnamed x2 -> x4, local copies, waits for them, and re-layouts: 0.01 us -> 4.87 us
  transfers between devices with their start and end apart: 7 -> 0, of which waited for: 5 -> 0; matrix products, arithmetic and copies ran while one was open for 0% -> 0% of each run, Pallas kernels for 0% -> 0%
where the time goes in v1:
time: 116 us
  Pallas kernels  108 us (93%)
  local copies, waits for them, and re-layouts  4.87 us (4%)
  between operations  3.05 us (3%)
    pallas_call x1, Pallas kernels, fused(): pl.pallas_call(kernel, out_shape=(jax.ShapeDtypeStruct((1, rows, hidden),...  108 us
    unnamed x4, local copies, waits for them, and re-layouts  4.87 us

profile of v1, /device:TPU:0, one launch (start us, length us, event | category | flops | bytes accessed | tf_op | source)
XLA Modules:
  0.0 115.8 jit_solution(8763552550268488906)
XLA Ops:
  1.3 107.9 %shard_map.49 = (f32[1,64,14336]{2,1,0:T(8,128)}, f32[64,896]{1,0:T(8,128)}, f32[1]{0:T(128)}) custom-call(bf16[1,64,14336]{2,1,0:T(8,128)(2,1)} %p_ref.1, s32[1]{0:T(128)S(6)} %copy.8.w_ref), custom_call_target="tpu_custom_call" | custom-call | tf_op jit(solution)/shard_map/pallas_call | solution.py:340
  109.2 0.0 copy-start
  109.2 4.2 %copy.9 = f32[1,64,14336]{2,1,0:T(8,128)} copy(f32[1,64,14336]{2,1,0:T(8,128)} %get-tuple-element.6) | data formatting | bytes 7340032
  113.4 0.0 copy-done
  113.4 0.7 copy.10
Async XLA Ops:
  109.2 4.2 %copy-start = (f32[64,896]{1,0:T(8,128)S(1)}, f32[64,896]{1,0:T(8,128)}, u32[]{:S(2)}) copy-start(f32[64,896]{1,0:T(8,128)} %get-tuple-element.7) | copy-start | bytes 688132

commit v2 on v1

--- a/solution.py
+++ b/solution.py
@@ -10,7 +10,7 @@
 ROUNDS = 3
 GROUP = 4
 LEVELS = 4
-SPLIT = 2
+SPLIT = 4
 LANES = 128
 
 
@@ -187,7 +187,14 @@
         for i in range(GROUP):
             acc[i] += sums[i]
 
+    def share(o):
+        return remote(acc.at[peer(o)], spread_in.at[o - 1], s_send.at[o - 1],
+                      s_recv.at[o - 1], dev(z, peer(o)))
+
     def send_back(k):
+        if k == chunks - 1:
+            for o in (2, 3, 1):
+                share(o).start()
         for o in (2, 3, 1):
             back(k, o).start()
         back_local(k).start()
@@ -265,8 +272,8 @@
             if 0 <= k < chunks:
                 across_relay(k).wait_recv()
                 finish(k, True)
+                outward_q(k, 1).start()
                 send_back(k)
-                outward_q(k, 1).start()
         for k in range(chunks):
             across(k).wait_send()
             across_relay(k).wait_send()
@@ -303,12 +310,6 @@
     average = pltpu.make_async_copy(avgbuf.at[z], avg_ref, avg_sem)
     average.start()
 
-    def share(o):
-        return remote(acc.at[peer(o)], spread_in.at[o - 1], s_send.at[o - 1],
-                      s_recv.at[o - 1], dev(z, peer(o)))
-
-    for o in (1, 2, 3):
-        share(o).start()
     for o in (1, 2, 3):
         share(o).wait_recv()
     spread_part[...] = acc[r] + spread_in[0] + spread_in[1] + spread_in[2]
@@ -344,7 +345,7 @@
             jax.ShapeDtypeStruct((rows, width), jnp.float32),
             jax.ShapeDtypeStruct((1,), jnp.float32),
         ),
-        in_specs=[pl.BlockSpec(memory_space=pl.ANY), pl.BlockSpec(memory_space=pltpu.SMEM)],
+        in_specs=[pl.BlockSpec(memory_space=pltpu.HBM), pl.BlockSpec(memory_space=pltpu.SMEM)],
         out_specs=(pl.BlockSpec(memory_space=pl.ANY), pl.BlockSpec(memory_space=pl.ANY),
                    pl.BlockSpec(memory_space=pltpu.SMEM)),
         scratch_shapes=[
@@ -362,7 +363,7 @@
             dma((8,)), dma((8,)), dma((4,)), dma((4,)), dma,
         ],
         compiler_params=pltpu.CompilerParams(
-            collective_id=0, has_side_effects=True, vmem_limit_bytes=56 << 20),
+            collective_id=0, has_side_effects=True, vmem_limit_bytes=20 << 20),
     )(params, weights)
     return debiased, average, spread
 

time: 116 us -> 110 us (0.948)
  Pallas kernels: 108 us -> 103 us
    pallas_call x1, Pallas kernels: 108 us -> 103 us  [fused(): pl.pallas_call(kernel, out_shape=(jax.ShapeDtypeStruct((1, rows, hidden),...]
where the time goes in v2:
time: 110 us
  Pallas kernels  103 us (94%)
  local copies, waits for them, and re-layouts  4.02 us (4%)
  between operations  3.06 us (3%)
    pallas_call x1, Pallas kernels, fused(): pl.pallas_call(kernel, out_shape=(jax.ShapeDtypeStruct((1, rows, hidden),...  103 us
    unnamed x4, local copies, waits for them, and re-layouts  4.02 us

profile of v2, /device:TPU:0, one launch (start us, length us, event | category | flops | bytes accessed | tf_op | source)
XLA Modules:
  0.0 109.9 jit_solution(3324977708778625230)
XLA Ops:
  1.3 0.0 copy-start
  1.3 1.5 %copy-done = bf16[1,64,14336]{2,1,0:T(8,128)(2,1)S(1)} copy-done((bf16[1,64,14336]{2,1,0:T(8,128)(2,1)S(1)}, bf16[1,64,14336]{2,1,0:T(8,128)(2,1)}, u32[]{:S(2)}) %copy-start) | copy-done | bytes 1835032
  2.8 102.9 %shard_map.49 = (f32[1,64,14336]{2,1,0:T(8,128)S(1)}, f32[64,896]{1,0:T(8,128)S(1)}, f32[1]{0:T(128)}) custom-call(bf16[1,64,14336]{2,1,0:T(8,128)(2,1)S(1)} %copy-done, s32[1]{0:T(128)S(6)} %copy.8.w_ref), custom_call_target="tpu_custom_call" | custom-call | tf_op jit(solution)/shard_map/pallas_call | solution.py:341
  105.6 1.8 %copy.9 = f32[1,64,14336]{2,1,0:T(8,128)} copy(f32[1,64,14336]{2,1,0:T(8,128)S(1)} %get-tuple-element.6) | data formatting | bytes 7340032
  107.5 0.7 copy.10
Async XLA Ops:
  1.3 1.5 %copy-start = (bf16[1,64,14336]{2,1,0:T(8,128)(2,1)S(1)}, bf16[1,64,14336]{2,1,0:T(8,128)(2,1)}, u32[]{:S(2)}) copy-start(bf16[1,64,14336]{2,1,0:T(8,128)(2,1)} %p_ref.1) | copy-start | bytes 5505028

commit v3 on v2

--- a/solution.py
+++ b/solution.py
@@ -12,13 +12,14 @@
 LEVELS = 4
 SPLIT = 4
 LANES = 128
+NEIGHBOUR = (1, 0, 3, 2)
 
 
 def kernel(p_ref, w_ref, out_ref, avg_ref, spread_ref,
            raw_own, raw_a, raw_b, raw_c, q_a, q_b, q_send, dbuf, avgbuf,
            wts, acc, spread_in, spread_part, spread_x,
            near_send, near_recv, own_sem, far_send, far_recv, back_send, back_recv,
-           back_own, w_send, w_recv, s_send, s_recv, avg_sem):
+           back_own, w_send, w_recv, s_send, s_recv, avg_sem, fore_in, f_send, f_recv):
     node = lax.axis_index("node")
     side = lax.axis_index("blk")
     z = node // GROUP
@@ -38,12 +39,10 @@
         return {"node": zz * GROUP + rr}
 
     inner = jnp.logical_and(z >= 1, z <= 2)
-    outer = jnp.logical_not(inner)
+    order = [k + half_of for k in range(chunks // 2) for half_of in (0, chunks // 2)]
     mate = 3 - z
     nb = (z // 2) * 2 + 1 - z % 2
     inner_count = (1 - z // 3) * ((z + 2) // 3)
-    opposite = (z + 2) % LEVELS
-    behind = (z + 3) % LEVELS
 
     def remote(src, dst, ssem, rsem, device):
         return pltpu.make_async_remote_copy(
@@ -92,7 +91,7 @@
 
     for o in (1, 2, 3):
         w_near(o).start()
-    for k in range(chunks):
+    for k in order:
         for o in (2, 3, 1):
             near(k, o).start()
 
@@ -132,93 +131,131 @@
     def group_weight(zz):
         return row(zz, 0) + row(zz, 1) + row(zz, 2) + row(zz, 3)
 
-    def finish(k, is_inner):
-        far = raw_c if is_inner else raw_a
-        at_one = (z == 1)
-        at_zero = (z == 0)
-        s0, s1 = row(z, 0), row(z, 0) + row(z, 1)
-        s2 = s1 + row(z, 2)
-        s3 = s2 + row(z, 3)
-        t3 = row(opposite, 3)
-        t2 = t3 + row(opposite, 2)
-        t1 = t2 + row(opposite, 1)
-        sb = group_weight(behind)
-        scales = (1.0 / (s0 + sb + t1), 1.0 / (s1 + sb + t2), 1.0 / (s2 + sb + t3),
-                  1.0 / (s3 + sb))
+    def scales_of(level):
+        opp = (level + 2) % LEVELS
+        sums = [group_weight((level + 3) % LEVELS)] * GROUP
+        for i in range(GROUP):
+            for e in range(GROUP):
+                if e <= i:
+                    sums[i] = sums[i] + row(level, e)
+                else:
+                    sums[i] = sums[i] + row(opp, e)
+        return [1.0 / value for value in sums]
+
+    def is_low(k):
+        return k < chunks // 2
+
+    def finish(k, level):
+        is_inner = level in (1, 2)
+        has_mean = is_low(k) == (level < 2)
+        opp, beside, across_level = (level + 2) % 4, NEIGHBOUR[level], 3 - level
+        if is_inner:
+            raws = {level: raw_own, beside: raw_a, across_level: raw_b, opp: raw_c}
+            group_refs = {}
+        else:
+            raws = {level: raw_own, opp: raw_a}
+            group_refs = {beside: q_a, across_level: q_b}
+        targets = [level]
+        if is_inner and has_mean:
+            targets += [across_level, opp]
+        scales = {y: scales_of(y) for y in targets}
         whole = 1.0 / (group_weight(0) + group_weight(1) + group_weight(2) + group_weight(3))
 
         def step(j, sums):
             cols = columns(j)
-            v0 = f32(raw_own, k, 0, cols) * row(z, 0)
-            v1 = v0 + f32(raw_own, k, 1, cols) * row(z, 1)
-            v2 = v1 + f32(raw_own, k, 2, cols) * row(z, 2)
-            v3 = v2 + f32(raw_own, k, 3, cols) * row(z, 3)
-            u3 = f32(far, k, 3, cols) * row(opposite, 3)
-            u2 = u3 + f32(far, k, 2, cols) * row(opposite, 2)
-            u1 = u2 + f32(far, k, 1, cols) * row(opposite, 1)
-            u0 = u1 + f32(far, k, 0, cols) * row(opposite, 0)
-            if is_inner:
-                q_send[k, 1, :, cols] = u0
-                qo = group_sum(raw_a, k, nb, cols)
-                qj = group_sum(raw_b, k, mate, cols)
-                prior = jnp.where(at_one, qo, qj)
-                total = v3 + u0 + qo + qj
-            else:
-                qi = q_a[k, :, cols]
-                qx = q_b[k, :, cols]
-                prior = jnp.where(at_zero, qx, qi)
-                total = v3 + u0 + qi + qx
-            mean = total * whole
-            avgbuf[k // SPLIT, own_slice(k), cols] = mean
+            seen = {}
+
+            def value(y, i):
+                if (y, i) not in seen:
+                    seen[y, i] = f32(raws[y], k, i, cols) * row(y, i)
+                return seen[y, i]
+
+            def group_of(y):
+                if y not in seen:
+                    if y in group_refs:
+                        seen[y] = group_refs[y][k, :, cols]
+                    else:
+                        seen[y] = (value(y, 0) + value(y, 1)) + (value(y, 2) + value(y, 3))
+                return seen[y]
+
+            if is_inner and sends_opposite(level, k):
+                q_send[k, 1, :, cols] = group_of(opp)
+            if has_mean:
+                mean = (group_of(0) + group_of(1) + group_of(2) + group_of(3)) * whole
+                avgbuf[k // SPLIT, own_slice(k), cols] = mean
             fresh = []
-            for i, value in enumerate((v0 + u1, v1 + u2, v2 + u3, v3)):
-                d = (value + prior) * scales[i]
-                dbuf[k, i, :, cols] = d
-                gap = d - mean
-                gap = gap * gap
-                part = gap[0:8]
-                for e in range(8, rows, 8):
-                    part = part + gap[e:e + 8]
-                fresh.append(sums[i] + part)
+            for n, y in enumerate(targets):
+                far = (y + 2) % LEVELS
+                prior = group_of((y + 3) % LEVELS)
+                heads = [value(y, 0)]
+                for i in range(1, GROUP):
+                    heads.append(heads[-1] + value(y, i))
+                tails = [None, None, None, value(far, 3)]
+                for i in (2, 1):
+                    tails[i] = tails[i + 1] + value(far, i)
+                for i in range(GROUP):
+                    d = heads[i] + prior
+                    if i + 1 < GROUP:
+                        d = d + tails[i + 1]
+                    d = d * scales[y][i]
+                    if n == 0:
+                        dbuf[k, i, :, cols] = d
+                    if has_mean:
+                        gap = d - mean
+                        gap = gap * gap
+                        part = gap[0:8]
+                        for e in range(8, rows, 8):
+                            part = part + gap[e:e + 8]
+                        fresh.append(sums[len(fresh)] + part)
             return tuple(fresh)
 
         zero = jnp.zeros((8, LANES), jnp.float32)
-        sums = lax.fori_loop(0, width // LANES, step, (zero,) * GROUP)
-        for i in range(GROUP):
-            acc[i] += sums[i]
+        count = GROUP * len(targets) if has_mean else 0
+        sums = lax.fori_loop(0, width // LANES, step, (zero,) * count)
+        for i in range(count):
+            acc[i // GROUP, i % GROUP] += sums[i]
 
     def share(o):
-        return remote(acc.at[peer(o)], spread_in.at[o - 1], s_send.at[o - 1],
+        return remote(acc.at[0, peer(o)], spread_in.at[o - 1], s_send.at[o - 1],
                       s_recv.at[o - 1], dev(z, peer(o)))
 
     def send_back(k):
-        if k == chunks - 1:
-            for o in (2, 3, 1):
-                share(o).start()
         for o in (2, 3, 1):
             back(k, o).start()
         back_local(k).start()
 
-    def to_inner(k):
+    def nodes(full):
+        return pl.ds(0, GROUP) if full else pl.ds(1, GROUP - 1)
+
+    def sends_opposite(level, k):
+        return level == 1 or not is_low(k)
+
+    def sends_own(level, k):
+        return level == 2 or is_low(k)
+
+    def to_inner(k, beside):
         return remote(raw_own.at[k], raw_a.at[k], far_send.at[k, 0], far_recv.at[k, 0],
-                      dev(nb, r))
-
-    def across(k):
-        return remote(raw_own.at[k], raw_b.at[k], far_send.at[k, 0], far_recv.at[k, 1],
-                      dev(mate, r))
-
-    def across_relay(k):
-        return remote(raw_a.at[k], raw_c.at[k], far_send.at[k, 1], far_recv.at[k, 2],
-                      dev(mate, r))
-
-    def outward_relay(k):
-        return remote(raw_b.at[k], raw_a.at[k], far_send.at[k, 2], far_recv.at[k, 0],
-                      dev(nb, r))
-
-    def outward_q(k, which):
+                      dev(beside, r))
+
+    def across(k, source):
+        part = nodes(source == 1 or is_low(k))
+        return remote(raw_own.at[k, part], raw_b.at[k, part], far_send.at[k, 0],
+                      far_recv.at[k, 1], dev(3 - source, r))
+
+    def across_relay(k, source):
+        part = nodes(source == 2 or not is_low(k))
+        return remote(raw_a.at[k, part], raw_c.at[k, part], far_send.at[k, 1],
+                      far_recv.at[k, 2], dev(3 - source, r))
+
+    def outward_relay(k, source):
+        part = nodes(is_low(k) == (source == 1))
+        return remote(raw_b.at[k, part], raw_a.at[k, part], far_send.at[k, 2],
+                      far_recv.at[k, 0], dev(NEIGHBOUR[source], r))
+
+    def outward_q(k, which, source):
         dst = q_b if which else q_a
         return remote(q_send.at[k, which], dst.at[k], far_send.at[k, 3 + which],
-                      far_recv.at[k, 3 + which], dev(nb, r))
+                      far_recv.at[k, 3 + which], dev(NEIGHBOUR[source], r))
 
     def w_copy(level, slot, target):
         return remote(wts.at[level], wts.at[level], w_send.at[slot], w_recv.at[slot],
@@ -228,91 +265,123 @@
         for o in (1, 2, 3):
             w_near(o).wait_recv()
 
-    @pl.when(inner)
-    def _():
+    def foreign(target):
+        return remote(acc.at[pl.ds(1, 2)], fore_in, f_send.at[0], f_recv.at[0],
+                      dev(target, r))
+
+    def foreign_relay(target):
+        return remote(fore_in.at[1], fore_in.at[0], f_send.at[1], f_recv.at[1],
+                      dev(target, r))
+
+    def inner_role(level):
+        beside, other, opp = NEIGHBOUR[level], 3 - level, (level + 2) % LEVELS
         arrived.clear()
 
         def group_out(k):
             wait_own(k)
+            if not sends_own(level, k):
+                return
 
             def step(j, carry):
                 cols = columns(j)
-                q_send[k, 0, :, cols] = group_sum(raw_own, k, z, cols)
+                q_send[k, 0, :, cols] = group_sum(raw_own, k, level, cols)
                 return carry
 
             lax.fori_loop(0, width // LANES, step, 0)
-            outward_q(k, 0).start()
+            outward_q(k, 0, level).start()
 
         wait_weights()
-        w_copy(z, 3, nb).start()
-        w_copy(z, 4, mate).start()
+        w_copy(level, 3, beside).start()
+        w_copy(level, 4, other).start()
         for t in range(chunks + 2):
             if t < chunks:
-                wait_own(t)
-                across(t).start()
-            for k in ((0,) if t == 0 else (2 * t - 1, 2 * t)):
-                if k < chunks:
-                    group_out(k)
+                wait_own(order[t])
+                across(order[t], level).start()
+            for e in ((0,) if t == 0 else (2 * t - 1, 2 * t)):
+                if e < chunks:
+                    group_out(order[e])
             if t == 1:
-                w_copy(nb, 3, nb).wait_recv()
-                w_copy(nb, 5, mate).start()
-                w_copy(z, 4, mate).wait_recv()
-                w_copy(mate, 6, nb).start()
-            k = t - 1
-            if 0 <= k < chunks:
-                across_in = to_inner(k)
-                across_in.wait_recv()
-                across_relay(k).start()
-                across(k).wait_recv()
-                outward_relay(k).start()
+                w_copy(beside, 3, beside).wait_recv()
+                w_copy(beside, 5, other).start()
+                w_copy(level, 4, other).wait_recv()
+                w_copy(other, 6, beside).start()
+            if 0 <= t - 1 < chunks:
+                k = order[t - 1]
+                to_inner(k, beside).wait_recv()
+                across_relay(k, level).start()
+                across(k, other).wait_recv()
+                outward_relay(k, level).start()
             if t == 2:
-                w_copy(nb, 5, mate).wait_recv()
-                w_copy(opposite, 7, nb).start()
-            k = t - 2
-            if 0 <= k < chunks:
-                across_relay(k).wait_recv()
-                finish(k, True)
-                outward_q(k, 1).start()
+                w_copy(opp, 5, other).wait_recv()
+                w_copy(opp, 7, beside).start()
+            if 0 <= t - 2 < chunks:
+                k = order[t - 2]
+                across_relay(k, other).wait_recv()
+                finish(k, level)
+                if sends_opposite(level, k):
+                    outward_q(k, 1, level).start()
+                if t == chunks + 1:
+                    foreign(other).start()
                 send_back(k)
-        for k in range(chunks):
-            across(k).wait_send()
-            across_relay(k).wait_send()
-            outward_relay(k).wait_send()
-            outward_q(k, 0).wait_send()
-            outward_q(k, 1).wait_send()
-        w_copy(z, 3, nb).wait_send()
-        w_copy(z, 4, mate).wait_send()
-        w_copy(nb, 5, mate).wait_send()
-        w_copy(mate, 6, nb).wait_send()
-        w_copy(opposite, 7, nb).wait_send()
-
-    @pl.when(outer)
-    def _():
+        foreign(other).wait_recv()
+        foreign_relay(beside).start()
+        acc[0] += fore_in[0]
+        for o in (1, 2, 3):
+            share(o).start()
+        for k in order:
+            across(k, level).wait_send()
+            across_relay(k, level).wait_send()
+            outward_relay(k, level).wait_send()
+            if sends_own(level, k):
+                outward_q(k, 0, level).wait_send()
+            if sends_opposite(level, k):
+                outward_q(k, 1, level).wait_send()
+        w_copy(level, 3, beside).wait_send()
+        w_copy(level, 4, other).wait_send()
+        w_copy(beside, 5, other).wait_send()
+        w_copy(other, 6, beside).wait_send()
+        w_copy(opp, 7, beside).wait_send()
+        foreign(other).wait_send()
+        foreign_relay(beside).wait_send()
+
+    def outer_role(level):
+        beside, other, opp = NEIGHBOUR[level], 3 - level, (level + 2) % LEVELS
         arrived.clear()
         wait_weights()
-        w_copy(z, 3, nb).start()
-        for k in range(chunks):
+        w_copy(level, 3, beside).start()
+        for k in order:
             wait_own(k)
-            to_inner(k).start()
-        w_copy(nb, 3, nb).wait_recv()
-        w_copy(opposite, 6, nb).wait_recv()
-        w_copy(mate, 7, nb).wait_recv()
-        for k in range(chunks):
-            outward_q(k, 0).wait_recv()
-            outward_relay(k).wait_recv()
-            outward_q(k, 1).wait_recv()
-            finish(k, False)
+            to_inner(k, beside).start()
+        w_copy(beside, 3, beside).wait_recv()
+        w_copy(opp, 6, beside).wait_recv()
+        w_copy(other, 7, beside).wait_recv()
+        for k in order:
+            if sends_own(beside, k):
+                outward_q(k, 0, beside).wait_recv()
+            outward_relay(k, beside).wait_recv()
+            if sends_opposite(beside, k):
+                outward_q(k, 1, beside).wait_recv()
+            finish(k, level)
+            if k == order[-1]:
+                foreign_relay(beside).wait_recv()
+                acc[0] += fore_in[0]
+                for o in (1, 2, 3):
+                    share(o).start()
             send_back(k)
-        for k in range(chunks):
-            to_inner(k).wait_send()
-        w_copy(z, 3, nb).wait_send()
+        for k in order:
+            to_inner(k, beside).wait_send()
+        w_copy(level, 3, beside).wait_send()
+
+    for level in range(LEVELS):
+        role = inner_role if level in (1, 2) else outer_role
+        pl.when(z == level)(functools.partial(role, level))
 
     average = pltpu.make_async_copy(avgbuf.at[z], avg_ref, avg_sem)
     average.start()
 
     for o in (1, 2, 3):
         share(o).wait_recv()
-    spread_part[...] = acc[r] + spread_in[0] + spread_in[1] + spread_in[2]
+    spread_part[...] = acc[0, r] + spread_in[0] + spread_in[1] + spread_in[2]
     swap = remote(spread_part, spread_x, s_send.at[3], s_recv.at[3], {"blk": 1 - side})
     swap.start()
     for k in range(chunks):
@@ -354,13 +423,14 @@
             pltpu.VMEM((chunks, GROUP, piece, width), jnp.float32),
             pltpu.VMEM((LEVELS, rows, width), jnp.float32),
             pltpu.VMEM((LEVELS, GROUP, 8, LANES), jnp.float32),
-            pltpu.VMEM((GROUP, 8, LANES), jnp.float32),
+            pltpu.VMEM((3, GROUP, 8, LANES), jnp.float32),
             pltpu.VMEM((3, 8, LANES), jnp.float32),
             tile, tile,
             dma((chunks, 3)), dma((chunks, 3)), dma((chunks,)),
             dma((chunks, 5)), dma((chunks, 5)),
             dma((chunks, 3)), dma((chunks, 3)), dma((chunks,)),
             dma((8,)), dma((8,)), dma((4,)), dma((4,)), dma,
+            pltpu.VMEM((2, GROUP, 8, LANES), jnp.float32), dma((2,)), dma((2,)),
         ],
         compiler_params=pltpu.CompilerParams(
             collective_id=0, has_side_effects=True, vmem_limit_bytes=20 << 20),

time: 110 us -> 107 us (0.973)
  Pallas kernels: 103 us -> 99.8 us
    pallas_call x1, Pallas kernels: 103 us -> 99.8 us  [fused(): pl.pallas_call(kernel, out_shape=(jax.ShapeDtypeStruct((1, rows, hidden),...]
where the time goes in v3:
time: 107 us
  Pallas kernels  99.8 us (93%)
  local copies, waits for them, and re-layouts  4.02 us (4%)
  between operations  3.06 us (3%)
    pallas_call x1, Pallas kernels, fused(): pl.pallas_call(kernel, out_shape=(jax.ShapeDtypeStruct((1, rows, hidden),...  99.8 us
    unnamed x4, local copies, waits for them, and re-layouts  4.02 us

profile of v3, /device:TPU:0, one launch (start us, length us, event | category | flops | bytes accessed | tf_op | source)
XLA Modules:
  0.0 106.9 jit_solution(11567871588676447809)
XLA Ops:
  1.3 0.0 copy-start
  1.3 1.5 %copy-done = bf16[1,64,14336]{2,1,0:T(8,128)(2,1)S(1)} copy-done((bf16[1,64,14336]{2,1,0:T(8,128)(2,1)S(1)}, bf16[1,64,14336]{2,1,0:T(8,128)(2,1)}, u32[]{:S(2)}) %copy-start) | copy-done | bytes 1835032
  2.8 99.8 %shard_map.49 = (f32[1,64,14336]{2,1,0:T(8,128)S(1)}, f32[64,896]{1,0:T(8,128)S(1)}, f32[1]{0:T(128)}) custom-call(bf16[1,64,14336]{2,1,0:T(8,128)(2,1)S(1)} %copy-done, s32[1]{0:T(128)S(6)} %copy.8.w_ref), custom_call_target="tpu_custom_call" | custom-call | tf_op jit(solution)/shard_map/pallas_call | solution.py:410
  102.6 1.8 %copy.9 = f32[1,64,14336]{2,1,0:T(8,128)} copy(f32[1,64,14336]{2,1,0:T(8,128)S(1)} %get-tuple-element.6) | data formatting | bytes 7340032
  104.4 0.7 copy.10
Async XLA Ops:
  1.3 1.5 %copy-start = (bf16[1,64,14336]{2,1,0:T(8,128)(2,1)S(1)}, bf16[1,64,14336]{2,1,0:T(8,128)(2,1)}, u32[]{:S(2)}) copy-start(bf16[1,64,14336]{2,1,0:T(8,128)(2,1)} %p_ref.1) | copy-start | bytes 5505028

commit v4 on v3

--- a/solution.py
+++ b/solution.py
@@ -294,9 +294,10 @@
         w_copy(level, 3, beside).start()
         w_copy(level, 4, other).start()
         for t in range(chunks + 2):
-            if t < chunks:
-                wait_own(order[t])
-                across(order[t], level).start()
+            for e in ((0, 1) if t == 0 else (t + 1,)):
+                if e < chunks:
+                    wait_own(order[e])
+                    across(order[e], level).start()
             for e in ((0,) if t == 0 else (2 * t - 1, 2 * t)):
                 if e < chunks:
                     group_out(order[e])

time: 107 us -> 107 us (level)
  no operation moved by 1% of the time
where the time goes in v4:
time: 107 us
  Pallas kernels  100 us (93%)
  local copies, waits for them, and re-layouts  4.02 us (4%)
  between operations  3.06 us (3%)
    pallas_call x1, Pallas kernels, fused(): pl.pallas_call(kernel, out_shape=(jax.ShapeDtypeStruct((1, rows, hidden),...  100 us
    unnamed x4, local copies, waits for them, and re-layouts  4.02 us

profile of v4, /device:TPU:0, one launch (start us, length us, event | category | flops | bytes accessed | tf_op | source)
XLA Modules:
  0.0 107.2 jit_solution(2559442689794795301)
XLA Ops:
  1.3 0.0 copy-start
  1.3 1.5 %copy-done = bf16[1,64,14336]{2,1,0:T(8,128)(2,1)S(1)} copy-done((bf16[1,64,14336]{2,1,0:T(8,128)(2,1)S(1)}, bf16[1,64,14336]{2,1,0:T(8,128)(2,1)}, u32[]{:S(2)}) %copy-start) | copy-done | bytes 1835032
  2.8 100.1 %shard_map.49 = (f32[1,64,14336]{2,1,0:T(8,128)S(1)}, f32[64,896]{1,0:T(8,128)S(1)}, f32[1]{0:T(128)}) custom-call(bf16[1,64,14336]{2,1,0:T(8,128)(2,1)S(1)} %copy-done, s32[1]{0:T(128)S(6)} %copy.8.w_ref), custom_call_target="tpu_custom_call" | custom-call | tf_op jit(solution)/shard_map/pallas_call | solution.py:411
  102.9 1.8 %copy.9 = f32[1,64,14336]{2,1,0:T(8,128)} copy(f32[1,64,14336]{2,1,0:T(8,128)S(1)} %get-tuple-element.6) | data formatting | bytes 7340032
  104.7 0.7 copy.10
Async XLA Ops:
  1.3 1.5 %copy-start = (bf16[1,64,14336]{2,1,0:T(8,128)(2,1)S(1)}, bf16[1,64,14336]{2,1,0:T(8,128)(2,1)}, u32[]{:S(2)}) copy-start(bf16[1,64,14336]{2,1,0:T(8,128)(2,1)} %p_ref.1) | copy-start | bytes 5505028
